TPU v7x, 128 devices: a whole 4x4x4 slice. The times are simulated.
128 devices in a mesh: dp: 8 (over y, x_lo), mp: 16 (over x_hi, z, core).
Axes of the slice: x: 4 (x_hi: 2, x_lo: 2; x = x_hi * 2 + x_lo), y: 4, z: 4, core: 2. Of those that a mesh axis runs over, the one named last changes fastest.
Arguments:
- tokens: bfloat16 [8, 2048, 5120], P('dp', 'mp'), may hold values from -6 to 6
- ln_gain: float32 [5120], replicated, may hold values from 0.1 to 1.9
- ln_bias: float32 [5120], replicated, may hold values from -3 to 3
- w_qkv: bfloat16 [5120, 3, 4096], P(None, None, 'mp'), may hold values from -0.15625 to 0.15625
- w_out: bfloat16 [4096, 5120], P('mp'), may hold values from -0.09375 to 0.09375
- grad_partial: bfloat16 [8, 4096, 5120], P('dp', 'mp'), may hold values from -6 to 6
Outputs:
- mixed: bfloat16 [8, 2048, 5120], P('dp', 'mp')
- grad_sum: float32 [4096, 5120], P('mp')
All inputs are finite; a program needn't handle non-finite values.
Results may differ from a plain program's by a relative error of at most 0.014.
The roundings to bfloat16 on the way count: a program that leaves them out, or rounds other values in their place, can miss the bound.
Values may be sent and summed in bfloat16 or wider, within the bound.
A program may use at most 192 MiB of HBM per device.

v0:
```python
import jax
import jax.numpy as jnp
from jax import lax
from jax.sharding import PartitionSpec as P

HEAD = 128
SEQ = 128


def layer_norm(rows, ln_gain, ln_bias):
    values = rows.astype(jnp.float32)
    center = jnp.mean(values, axis=-1, keepdims=True)
    spread = jnp.mean((values - center) * (values - center), axis=-1, keepdims=True)
    return ((values - center) * lax.rsqrt(spread + 1e-06) * ln_gain + ln_bias).astype(jnp.bfloat16)


def body(tokens, ln_gain, ln_bias, w_qkv, w_out, grad_partial):
    local_rows = tokens[0]
    inner_dev = w_qkv.shape[2]
    heads_dev = inner_dev // HEAD
    weight_flat = w_qkv.reshape(w_qkv.shape[0], 3 * inner_dev)
    normed_local = layer_norm(local_rows, ln_gain, ln_bias)
    qkv = jnp.dot(
        lax.all_gather(normed_local, "mp", axis=0, tiled=True),
        weight_flat,
        preferred_element_type=jnp.float32,
    ).astype(jnp.bfloat16)
    images = qkv.shape[0] // SEQ
    query = qkv[:, :inner_dev].reshape(images, SEQ, heads_dev, HEAD)
    keys = qkv[:, inner_dev : 2 * inner_dev].reshape(images, SEQ, heads_dev, HEAD)
    values = qkv[:, 2 * inner_dev :].reshape(images, SEQ, heads_dev, HEAD)
    scores = jnp.einsum(
        "bqhd,bkhd->bhqk", query, keys, preferred_element_type=jnp.float32
    ) * HEAD ** (-0.5)
    scaled = scores - jnp.max(scores, axis=-1, keepdims=True)
    expsc = jnp.exp(scaled)
    attn = (expsc / jnp.sum(expsc, axis=-1, keepdims=True)).astype(jnp.bfloat16)
    context = jnp.einsum(
        "bhqk,bkhd->bqhd", attn, values, preferred_element_type=jnp.float32
    ).astype(jnp.bfloat16)
    context = context.reshape(images * SEQ, inner_dev)
    partial_sum = jnp.dot(context, w_out, preferred_element_type=jnp.float32).astype(jnp.bfloat16)
    partial_sum = lax.optimization_barrier(partial_sum)
    proj = lax.psum_scatter(
        partial_sum.astype(jnp.float32).astype(jnp.bfloat16), "mp", scatter_dimension=0, tiled=True
    ).astype(jnp.float32)
    mixed = (local_rows.astype(jnp.float32) + proj).astype(jnp.bfloat16)[None]
    grad_sum = lax.psum(grad_partial[0], "dp").astype(jnp.float32)
    return (mixed, grad_sum)


def solution(mesh):
    placed = (
        P("dp", "mp", None),
        P(),
        P(),
        P(None, None, "mp"),
        P("mp", None),
        P("dp", "mp", None),
    )
    return jax.shard_map(
        body,
        mesh=mesh,
        in_specs=placed,
        out_specs=(P("dp", "mp", None), P("mp", None)),
        check_vma=False,
    )
```

profile of v0, /device:TPU:0, one launch (start us, length us, event | category | flops | bytes accessed | tf_op | source)
XLA Modules:
  0.0 383.3 jit_solution(12691280040116896814)
XLA Ops:
  8.0 0.0 all-gather.2.cloned.1.call-start
  8.1 1.7 convert_reduce_fusion
  9.8 1.8 fusion.5
  11.7 1.6 fusion.8
  13.3 0.0 all-gather.2.cloned.1.call-update
  13.4 0.0 all-reduce.2.cloned.1.call-start
  13.4 0.5 all-reduce.2.cloned.1.call-update
  13.9 0.0 reduce-scatter.2.cloned.1.call-start
  14.0 10.7 %copy.12 = bf16[5120,3,256]{0,2,1:T(8,128)(2,1)} copy(bf16[5120,3,256]{2,0,1:T(8,128)(2,1)} %param.9) | data formatting | bytes 15728640 | tf_op args[3]
  24.7 128.7 %all-gather.2.cloned.1.call-done = bf16[2048,5120]{1,0:T(8,128)(2,1)} async-done(((bf16[128,5120]{1,0:T(8,128)(2,1)}), bf16[2048,5120]{1,0:T(8,128)(2,1)}) %all-gather.2.cloned.1.call-update) | async-done | bytes 20971536 | tf_op jit(solution)/shard_map/all_gather | solution.py:24
  153.4 21.9 %convolution_convert_fusion.1 = bf16[2048,768]{1,0:T(8,128)(2,1)S(1)} fusion(bf16[2048,5120]{1,0:T(8,128)(2,1)} %all-gather.2.cloned.1.call-done, bf16[5120,768]{0,1:T(8,128)(2,1)} %bitcast.38), kind=kOutput, calls=%fused_computation.2 | convolution fusion | flops 16107700224 | bytes 31981568 | tf_op jit(solution)/shard_map/dot_general | solution.py:23
  175.3 1.7 fusion.37
  177.1 2.2 reshape.38
  179.2 2.2 reshape.39
  181.4 2.1 reshape.37
  183.6 2.5 fusion.38
  186.1 3.7 fusion.16
  189.8 3.9 %fusion.11 = bf16[16,128,2,128]{1,3,2,0:T(8,128)(2,1)} fusion(bf16[16,128,2,128]{3,2,1,0:T(2,128)(2,1)} %reshape.37, f32[16,2,128]{2,1,0:T(2,128)S(1)} %fusion.38, f32[16,2,128,128]{2,3,1,0:T(8,128)} %fusion.16), kind=kOutput, calls=%fused_computation.19 | convolution fusion | flops 136843392 | bytes 4210688 | tf_op jit(solution)/shard_map/bhqk,bkhd->bqhd/dot_general | solution.py:38
  193.7 1.9 copy.17
  195.7 10.1 %convolution_convert_fusion = bf16[2048,5120]{1,0:T(8,128)(2,1)} fusion(bf16[256,5120]{1,0:T(8,128)(2,1)S(1)} %copy-done, bf16[32,8,16,128]{3,2,1,0:T(8,128)(2,1)S(1)} %bitcast.39), kind=kOutput, calls=%fused_computation.1 | convolution fusion | flops 5379194880 | bytes 24641536 | tf_op jit(solution)/shard_map/dot_general | solution.py:42
  205.8 7.4 %all-reduce.2.cloned.1.call-done = bf16[256,5120]{1,0:T(8,128)(2,1)} async-done(((bf16[256,5120]{1,0:T(8,128)(2,1)}), bf16[256,5120]{1,0:T(8,128)(2,1)}) %all-reduce.2.cloned.1.call-update) | async-done | bytes 2621456 | tf_op jit(solution)/shard_map/psum | solution.py:48
  213.1 5.7 %convert_element_type.46 = f32[256,5120]{1,0:T(8,128)} convert(bf16[256,5120]{1,0:T(8,128)(2,1)} %all-reduce.2.cloned.1.call-done) | non-fusion elementwise | flops 1310720 | bytes 7864320 | tf_op jit(solution)/shard_map/convert_element_type | solution.py:48
  218.9 153.9 %reduce-scatter.2.cloned.1.call-done = bf16[128,5120]{1,0:T(8,128)(2,1)} async-done(((bf16[2048,5120]{1,0:T(8,128)(2,1)}), bf16[128,5120]{1,0:T(8,128)(2,1)}) %reduce-scatter.2.cloned.1.call-update) | async-done | bytes 1310736 | tf_op jit(solution)/shard_map/reduce_scatter | solution.py:44
  372.8 3.1 fusion.12
  (11 shorter events, 0.1 us)
Async XLA Ops:
  8.0 187.7 %copy-start = (bf16[256,5120]{1,0:T(8,128)(2,1)S(1)}, bf16[256,5120]{1,0:T(8,128)(2,1)}, u32[]{:S(2)}) copy-start(bf16[256,5120]{1,0:T(8,128)(2,1)} %param.10) | copy-start | bytes 7864324
  8.0 3.6 copy-start.3
  8.0 3.6 copy-start.2
  8.0 145.4 %all-gather.2.cloned.1.call-start = ((), (), s32[]{:S(2)}) async-start(), calls=%async_computation.1 | async-start | bytes 22282240 | tf_op jit(solution)/shard_map/all_gather | solution.py:24
  8.1 3.6 copy-start.1
  13.4 199.8 %all-reduce.2.cloned.1.call-start = ((), (), s32[]{:S(2)}) async-start(), calls=%async_computation.3 | async-start | bytes 5242880 | tf_op jit(solution)/shard_map/psum | solution.py:48
  13.9 358.9 %reduce-scatter.2.cloned.1.call-start = ((), (), s32[]{:S(2)}) async-start(), calls=%async_computation.2 | async-start | bytes 22282240 | tf_op jit(solution)/shard_map/reduce_scatter | solution.py:44
Sparse Core Ops, SparseCore 0:
  13.5 139.8 all-gather.1
  205.9 166.8 reduce-scatter.1
Sparse Core Ops, SparseCore 1:
  16.4 196.7 all-reduce.1
where the time goes:
time: 384 us; the launch traced here: 383 us
  waiting for transfers between devices  291 us (76%)
  matrix products  42.1 us (11%)
  local copies, waits for them, and re-layouts  20.9 us (5%)
  between operations  15.6 us (4%)
  other arithmetic  14 us (4%)
    reduce_scatter x1, waiting for transfers between devices, body(): lax.psum_scatter(partial_sum.astype(jnp.float32).astype(jnp.bfloat16), 'm...  154 us
    all_gather x1, waiting for transfers between devices, body(): lax.all_gather(normed_local, 'mp', axis=0, tiled=True)  129 us
    dot_general x1, matrix products, body(): jnp.dot(lax.all_gather(normed_local, 'mp', axis=0, tiled=True), weight_fl...  21.9 us
    unnamed x9, local copies, waits for them, and re-layouts  10.8 us
    dot_general x1, matrix products, body(): jnp.dot(context, w_out, preferred_element_type=jnp.float32)  10.1 us
  transfers between devices with their start and end apart: 3, of which 3 were waited for; matrix products, arithmetic and copies ran while one was open for 18% of the time, Pallas kernels for 0%

commit v1 on v0

v1 whole, which is shorter than its diff:
```python
import jax
import jax.numpy as jnp
from jax import lax
from jax.experimental import pallas as pl
from jax.experimental.pallas import tpu as pltpu
from jax.sharding import PartitionSpec as P

HEAD = 128
SEQ = 128
D = 5120
NY = 4
NZ = 4
WIDTH = 256
HALF = SEQ // 2
QUART = SEQ // 4
GROWS = WIDTH // NY
MESH = pl.DeviceIdType.MESH
BF = jnp.bfloat16
F32 = jnp.float32


def attend(query, keys, values):
    scores = lax.dot_general(
        query, keys, (((1,), (1,)), ((), ())), preferred_element_type=F32
    ) * HEAD ** (-0.5)
    scaled = scores - jnp.max(scores, axis=-1, keepdims=True)
    expsc = jnp.exp(scaled)
    attn = (expsc / jnp.sum(expsc, axis=-1, keepdims=True)).astype(BF)
    return jnp.dot(attn, values, preferred_element_type=F32).astype(BF)


def kernel(
    tok_hbm, gain, bias, wq_hbm, wo_hbm, g_hbm,
    mixed_hbm, gsum_hbm,
    raw, T, WQ, WO, QKV, CTX, CTXR, PS, RB,
    GO, GR, GX, GXR, GT, GA, GF, OM,
    zs, zr, xs, xr, cs, cr, rss, rsr,
    wqs, wqr, wos, wor, gs, gr, loc, outs,
):
    dp = lax.axis_index("dp")
    mp = lax.axis_index("mp")
    y, xl = dp // 2, dp % 2
    xh, z, c = mp // 8, (mp // 2) % 4, mp % 2

    def dev(y, xl, xh, z, c):
        return (lax.rem(y + NY, NY) * 2 + xl, xh * 8 + lax.rem(z + NZ, NZ) * 2 + c)

    zdev = (dev(y, xl, xh, z + 1, c), dev(y, xl, xh, z - 1, c))
    x2 = dev(y, xl, 1 - xh, z, c)
    mate = dev(y, xl, xh, z, 1 - c)
    cross = dev(y, 1 - xl, 1 - xh, z, c)
    xlo = dev(y, 1 - xl, xh, z, c)
    ydev = [dev(y + k, xl, xh, z, c) for k in (1, 2, 3 - NY)]

    def local(src, dst, sem):
        copy = pltpu.make_async_copy(src, dst, sem)
        copy.start()
        return copy

    load_raw = local(tok_hbm, raw, loc.at[0])
    load_wq = [local(wq_hbm.at[j], WQ.at[c * 3 + j], loc.at[1 + j]) for j in range(3)]
    own_seg = pl.multiple_of((xh * 2 + c) * WIDTH, WIDTH)
    far_seg = pl.multiple_of(((1 - xh) * 2 + c) * WIDTH, WIDTH)
    load_wo = local(wo_hbm, WO.at[pl.ds(own_seg, WIDTH)], loc.at[4])
    my_rows = pl.ds(pl.multiple_of(y * GROWS, GROWS), GROWS)
    load_g = local(g_hbm.at[my_rows], GO, loc.at[5])

    barrier = pltpu.get_barrier_semaphore()
    peers = [*zdev, x2, mate, cross, xlo, *ydev]
    for peer in peers:
        pl.semaphore_signal(barrier, inc=1, device_id=peer, device_id_type=MESH)
    pl.semaphore_wait(barrier, len(peers))

    sent = []

    def send(src, dst, ssem, rsem, peer):
        copy = pltpu.make_async_remote_copy(
            src_ref=src, dst_ref=dst, send_sem=ssem, recv_sem=rsem,
            device_id=peer, device_id_type=MESH,
        )
        copy.start()
        sent.append(copy)
        return copy

    wo_cross = send(
        wo_hbm.at[my_rows], WO.at[pl.ds(own_seg + y * GROWS, GROWS)],
        wos.at[0], wor.at[0], cross,
    )
    wq_mate = [
        send(wq_hbm.at[j], WQ.at[c * 3 + j], wqs.at[j], wqr.at[j], mate) for j in range(3)
    ]
    wo_mate = send(wo_hbm, WO.at[pl.ds(own_seg, WIDTH)], wos.at[1], wor.at[1], mate)
    g_rs = []
    for k in range(3):
        rows = pl.ds(pl.multiple_of(lax.rem(y + k + 1, NY) * GROWS, GROWS), GROWS)
        g_rs.append(send(g_hbm.at[rows], GR.at[k], gs.at[k], gr.at[k], ydev[k]))

    def slot(col, zz):
        return col * NZ + lax.rem(zz + 2 * NZ, NZ)

    def quarter(h, q):
        return pl.ds(h * HALF + q * QUART, QUART)

    zcopy, xcopy = {}, {}

    def zsend(step, h, q, s):
        ref = T.at[s, quarter(h, q)]
        zcopy[step, h, q] = send(ref, ref, zs.at[h, step, q], zr.at[h, step, q], zdev[h])

    def xsend(step, h, q, s):
        ref = T.at[s, quarter(h, q)]
        xcopy[step, h, q] = send(ref, ref, xs.at[step, h, q], xr.at[step, h, q], x2)

    sign = (1, -1)
    own = slot(xh, z)

    load_raw.wait()
    for q in range(2):
        for h in range(2):
            @pl.loop(0, QUART // 16)
            def _(i, h=h, q=q):
                rows = pl.ds(pl.multiple_of(h * HALF + q * QUART + i * 16, 16), 16)
                values = raw[rows, :].astype(F32)
                center = jnp.mean(values, axis=-1, keepdims=True)
                spread = jnp.mean((values - center) * (values - center), axis=-1, keepdims=True)
                T[own, rows, :] = (
                    (values - center) * lax.rsqrt(spread + 1e-06) * gain[...] + bias[...]
                ).astype(BF)
            zsend(0, h, q, own)
            xsend(0, h, q, own)

    def project(s, base, count):
        @pl.loop(0, count)
        def _(j):
            QKV[base + j] = jnp.dot(T[s], WQ[base + j], preferred_element_type=F32).astype(BF)

    def attention(s):
        for cc in range(2):
            for h in range(2):
                cols = slice(h * HEAD, (h + 1) * HEAD)
                CTX[s, :, cc * WIDTH + h * HEAD:cc * WIDTH + (h + 1) * HEAD] = attend(
                    QKV[cc * 3, :, cols], QKV[cc * 3 + 1, :, cols], QKV[cc * 3 + 2, :, cols]
                )

    ccopy = {}

    def ctx_send(k):
        zz = lax.rem(z + k, NZ)
        ccopy[k] = send(CTX.at[slot(1 - xh, z + k)], CTXR.at[zz], cs.at[k], cr.at[k], x2)

    for copy in load_wq:
        copy.wait()
    project(own, c * 3, 3)
    for h in range(2):
        zcopy[0, h, 0].wait_recv()
        zsend(1, h, 0, slot(xh, z - sign[h]))
    for copy in wq_mate:
        copy.wait_recv()
    project(own, (1 - c) * 3, 3)
    attention(own)
    for h in range(2):
        zcopy[0, h, 1].wait_recv()
        zsend(1, h, 1, slot(xh, z - sign[h]))

    wo_cross.wait_recv()
    far_rows = WO.at[pl.ds(far_seg + y * GROWS, GROWS)]
    wo_y = [send(far_rows, far_rows, wos.at[2 + k], wor.at[2 + k], ydev[k]) for k in range(3)]
    wo_fwd = [send(far_rows, far_rows, wos.at[5], wor.at[5], mate)]

    for q in range(2):
        for h in range(2):
            zcopy[1, h, q].wait_recv()
            zsend(2, h, q, slot(xh, z + 2))
            xsend(1, h, q, slot(xh, z + 2))
    for q in range(2):
        for h in range(2):
            xcopy[0, h, q].wait_recv()
            zsend(3, h, q, slot(1 - xh, z))

    @pl.loop(0, 2)
    def _(i):
        s = jnp.where(i == 0, slot(1 - xh, z), slot(xh, z + 2))
        project(s, 0, 6)
        attention(s)
    ctx_send(0)

    for q in range(2):
        for h in range(2):
            zcopy[2, h, q].wait_recv()
    for h in range(2):
        xcopy[1, h, 0].wait_recv()
        zsend(4, h, 0, slot(1 - xh, z + 2))

    @pl.loop(0, 2)
    def _(i):
        s = slot(xh, z + 1 + 2 * i)
        project(s, 0, 6)
        attention(s)

    for h in range(2):
        xcopy[1, h, 1].wait_recv()
        zsend(4, h, 1, slot(1 - xh, z + 2))

    def by_rows(count, fn):
        @pl.loop(0, count // 16)
        def _(i):
            fn(pl.ds(pl.multiple_of(i * 16, 16), 16))

    load_g.wait()
    for copy in g_rs:
        copy.wait_recv()

    def sum4(rows):
        GX[rows, :] = (
            (GO[rows, :].astype(F32) + GR[0, rows, :].astype(F32))
            + (GR[1, rows, :].astype(F32) + GR[2, rows, :].astype(F32))
        ).astype(BF)
    by_rows(GROWS, sum4)
    g_x = send(GX, GXR, gs.at[3], gr.at[3], xlo)

    for k in range(3):
        wo_y[k].wait_recv()
        rows = WO.at[pl.ds(far_seg + lax.rem(y + NY - k - 1, NY) * GROWS, GROWS)]
        wo_fwd.append(send(rows, rows, wos.at[6 + k], wor.at[6 + k], mate))

    project(slot(1 - xh, z + 2), 0, 6)
    attention(slot(1 - xh, z + 2))
    ctx_send(2)

    load_wo.wait()
    wo_mate.wait_recv()
    for copy in wo_fwd:
        copy.wait_recv()

    def out_project(k):
        zz = lax.rem(z + k, NZ)
        near = pl.ds(pl.multiple_of(xh * 2 * WIDTH, WIDTH), 2 * WIDTH)
        far = pl.ds(pl.multiple_of((1 - xh) * 2 * WIDTH, WIDTH), 2 * WIDTH)

        @pl.loop(0, D // 512)
        def _(j):
            cols = pl.ds(pl.multiple_of(j * 512, 512), 512)
            PS[zz, :, cols] = (
                jnp.dot(CTX[slot(xh, zz)], WO[near, cols], preferred_element_type=F32)
                + jnp.dot(CTXR[zz], WO[far, cols], preferred_element_type=F32)
            ).astype(BF)

    ccopy[0].wait_recv()
    out_project(0)

    g_x.wait_recv()

    def sum2(rows):
        GT[rows, :] = (GX[rows, :].astype(F32) + GXR[rows, :].astype(F32)).astype(BF)
    by_rows(GROWS, sum2)
    g_ag = [send(GT, GA.at[k], gs.at[4 + k], gr.at[4 + k], ydev[k]) for k in range(3)]

    ccopy[2].wait_recv()
    out_project(2)

    rcopy = {}

    def rsend(kind, q, image, h, to):
        ref = PS.at[lax.rem(image + 2 * NZ, NZ), quarter(h, q)]
        rcopy[kind, q] = send(
            ref, RB.at[kind, pl.ds(q * QUART, QUART)],
            rss.at[kind, q], rsr.at[kind, q], zdev[to],
        )

    for q in range(2):
        rsend(0, q, z + 2, 0, 1)
        rsend(1, q, z + 2, 1, 0)

    for q in range(2):
        for h in range(2):
            zcopy[3, h, q].wait_recv()
            zcopy[4, h, q].wait_recv()
    for k in (1, 3):
        project(slot(1 - xh, z + k), 0, 6)
        attention(slot(1 - xh, z + k))
        ctx_send(k)
    ccopy[1].wait_recv()
    out_project(1)
    for q in range(2):
        rsend(4, q, z + 1, 0, 0)
    ccopy[3].wait_recv()
    out_project(3)
    for q in range(2):
        rsend(5, q, z - 1, 1, 1)

    for q in range(2):
        for h in range(2):
            image = lax.rem(z - sign[h] + NZ, NZ)
            rcopy[h, q].wait_recv()

            @pl.loop(0, QUART // 16)
            def _(i, h=h, q=q, image=image):
                at = pl.multiple_of(q * QUART + i * 16, 16)
                rows = pl.ds(h * HALF + at, 16)
                PS[image, rows, :] = (
                    PS[image, rows, :].astype(F32) + RB[h, pl.ds(at, 16), :].astype(F32)
                ).astype(BF)
            rsend(2 + h, q, z - sign[h], h, 1 - h)

    written = []
    for k in range(4):
        if k:
            g_ag[k - 1].wait_recv()
        if k >= 2:
            written[k - 2].wait()

        def widen(rows, k=k):
            part = GT[rows, :] if k == 0 else GA[k - 1, rows, :]
            GF[k % 2, rows, :] = part.astype(F32)
        by_rows(GROWS, widen)
        rows = pl.ds(pl.multiple_of(lax.rem(y + NY - k, NY) * GROWS, GROWS), GROWS)
        written.append(local(GF.at[k % 2], gsum_hbm.at[rows], outs.at[k]))

    for q in range(2):
        for h in range(2):
            rcopy[4 + h, q].wait_recv()
            rcopy[2 + h, q].wait_recv()

            @pl.loop(0, QUART // 16)
            def _(i, h=h, q=q):
                at = pl.multiple_of(q * QUART + i * 16, 16)
                rows = pl.ds(h * HALF + at, 16)
                part = pl.ds(at, 16)
                proj = PS[z, rows, :].astype(F32) + (
                    RB[2 + h, part, :].astype(F32) + RB[4 + h, part, :].astype(F32)
                )
                OM[rows, :] = (raw[rows, :].astype(F32) + proj).astype(BF)
            written.append(
                local(OM.at[quarter(h, q)], mixed_hbm.at[quarter(h, q)], outs.at[4 + h * 2 + q])
            )
    for copy in written[2:]:
        copy.wait()
    for copy in sent:
        copy.wait_send()


def body(tokens, ln_gain, ln_bias, w_qkv, w_out, grad_partial):
    dma = pltpu.SemaphoreType.DMA
    any_spec = pl.BlockSpec(memory_space=pl.ANY)
    vmem = pl.BlockSpec(memory_space=pltpu.VMEM)
    mixed, grad_sum = pl.pallas_call(
        kernel,
        out_shape=(
            jax.ShapeDtypeStruct((SEQ, D), BF),
            jax.ShapeDtypeStruct((WIDTH, D), F32),
        ),
        in_specs=[any_spec, vmem, vmem, any_spec, any_spec, any_spec],
        out_specs=(any_spec, any_spec),
        scratch_shapes=[
            pltpu.VMEM((SEQ, D), BF),
            pltpu.VMEM((2 * NZ, SEQ, D), BF),
            pltpu.VMEM((6, D, WIDTH), BF),
            pltpu.VMEM((4 * WIDTH, D), BF),
            pltpu.VMEM((6, SEQ, WIDTH), BF),
            pltpu.VMEM((2 * NZ, SEQ, 2 * WIDTH), BF),
            pltpu.VMEM((NZ, SEQ, 2 * WIDTH), BF),
            pltpu.VMEM((NZ, SEQ, D), BF),
            pltpu.VMEM((6, HALF, D), BF),
            pltpu.VMEM((GROWS, D), BF),
            pltpu.VMEM((3, GROWS, D), BF),
            pltpu.VMEM((GROWS, D), BF),
            pltpu.VMEM((GROWS, D), BF),
            pltpu.VMEM((GROWS, D), BF),
            pltpu.VMEM((3, GROWS, D), BF),
            pltpu.VMEM((2, GROWS, D), F32),
            pltpu.VMEM((SEQ, D), BF),
            dma((2, 5, 2)), dma((2, 5, 2)),
            dma((2, 2, 2)), dma((2, 2, 2)),
            dma((4,)), dma((4,)),
            dma((6, 2)), dma((6, 2)),
            dma((3,)), dma((3,)),
            dma((9,)), dma((9,)),
            dma((7,)), dma((7,)),
            dma((6,)), dma((8,)),
        ],
        compiler_params=pltpu.CompilerParams(
            collective_id=0, has_side_effects=True, vmem_limit_bytes=67043328
        ),
    )(
        tokens[0], ln_gain[None], ln_bias[None],
        jnp.transpose(w_qkv, (1, 0, 2)), w_out, grad_partial[0],
    )
    return (mixed[None], grad_sum)


def solution(mesh):
    placed = (
        P("dp", "mp", None),
        P(),
        P(),
        P(None, None, "mp"),
        P("mp", None),
        P("dp", "mp", None),
    )
    return jax.shard_map(
        body,
        mesh=mesh,
        in_specs=placed,
        out_specs=(P("dp", "mp", None), P("mp", None)),
        check_vma=False,
    )
```

time: 384 us -> 160 us (0.42)
  waiting for transfers between devices: 291 us -> 0 us
  Pallas kernels: 0 us -> 151 us
  matrix products: 42.1 us -> 0 us
  between operations: 15.6 us -> 0.64 us
  other arithmetic: 14 us -> 0 us
  local copies, waits for them, and re-layouts: 20.9 us -> 7.87 us
    reduce_scatter x1 -> x0, waiting for transfers between devices: 154 us -> none  [body(): lax.psum_scatter(partial_sum.astype(jnp.float32).astype(jnp.bfloat16), 'm...]
    pallas_call x0 -> x1, Pallas kernels: none -> 151 us  [body(): pl.pallas_call(kernel, out_shape=(jax.ShapeDtypeStruct((SEQ, D), BF), jax...]
    all_gather x1 -> x0, waiting for transfers between devices: 129 us -> none  [body(): lax.all_gather(normed_local, 'mp', axis=0, tiled=True)]
    dot_general x4 -> x0, matrix products: 39.6 us -> none  [the longest x1 21.9 us: body(): jnp.dot(lax.all_gather(normed_local, 'mp', axis=0, tiled=True), weight_fl...]
    convert_element_type x2 -> x0, other arithmetic: 7.38 us -> none  [the longest x1 5.74 us: body(): grad_sum = lax.psum(grad_partial[0], 'dp').astype(jnp.float32)]
    psum x1 -> x0, waiting for transfers between devices: 7.35 us -> none  [body(): grad_sum = lax.psum(grad_partial[0], 'dp').astype(jnp.float32)]
    reshape x3 -> x0, local copies, waits for them, and re-layouts: 6.49 us -> none  [the longest x1 2.2 us: body(): keys = qkv[:, inner_dev:2 * inner_dev].reshape(images, SEQ, heads_dev, HEAD)]
    unnamed x9 -> x2, local copies, waits for them, and re-layouts: 10.8 us -> 7.87 us
  transfers between devices with their start and end apart: 3 -> 0, of which waited for: 3 -> 0; matrix products, arithmetic and copies ran while one was open for 18% -> 0% of each run, Pallas kernels for 0% -> 0%
where the time goes in v1:
time: 160 us; the launch traced here: 159 us
  Pallas kernels  151 us (94%)
  local copies, waits for them, and re-layouts  7.87 us (5%)
    pallas_call x1, Pallas kernels, body(): pl.pallas_call(kernel, out_shape=(jax.ShapeDtypeStruct((SEQ, D), BF), jax...  151 us
    unnamed x2, local copies, waits for them, and re-layouts  7.87 us

profile of v1, /device:TPU:0, one launch (start us, length us, event | category | flops | bytes accessed | tf_op | source)
XLA Modules:
  0.0 159.3 jit_solution(2596169219542920099)
XLA Ops:
  0.6 150.8 %shard_map.77 = (bf16[128,5120]{1,0:T(8,128)(2,1)}, f32[256,5120]{1,0:T(8,128)}) custom-call(bf16[128,5120]{1,0:T(8,128)(2,1)} %bitcast.8, f32[1,5120]{1,0:T(1,128)} %bitcast.10, f32[1,5120]{1,0:T(1,128)} %bitcast.11, bf16[3,5120,256]{2,1,0:T(8,128)(2,1)} %bitcast.6, bf16[256,5120]{1,0:T(8,128)(2,1)} %wo_hbm.1, bf16[256,5120]{1,0:T(8,128)(2,1)} %bitcast.7), custom_call_target="tpu_custom_call" | custom-call | tf_op jit(solution)/shard_map/pallas_call | solution.py:346
  151.5 2.5 %copy.10 = bf16[1,128,5120]{2,1,0:T(8,128)(2,1)} copy(bf16[1,128,5120]{2,1,0:T(8,128)(2,1)} %bitcast.9) | data formatting | bytes 2621440
  153.9 5.4 %copy.11 = f32[256,5120]{1,0:T(8,128)} copy(f32[256,5120]{1,0:T(8,128)} %get-tuple-element.9) | data formatting | bytes 10485760

commit v2 on v1

--- a/solution.py
+++ b/solution.py
@@ -33,7 +33,7 @@
     tok_hbm, gain, bias, wq_hbm, wo_hbm, g_hbm,
     mixed_hbm, gsum_hbm,
     raw, T, WQ, WO, QKV, CTX, CTXR, PS, RB,
-    GO, GR, GX, GXR, GT, GA, GF, OM,
+    GO, GR, GX, GXR, GT, GA, OM,
     zs, zr, xs, xr, cs, cr, rss, rsr,
     wqs, wqr, wos, wor, gs, gr, loc, outs,
 ):
@@ -69,6 +69,23 @@
     peers = [*zdev, x2, mate, cross, xlo, *ydev]
     for peer in peers:
         pl.semaphore_signal(barrier, inc=1, device_id=peer, device_id_type=MESH)
+
+    def slot(col, zz):
+        return col * NZ + lax.rem(zz + 2 * NZ, NZ)
+
+    own = slot(xh, z)
+    load_raw.wait()
+
+    @pl.loop(0, SEQ // 16)
+    def _(i):
+        rows = pl.ds(pl.multiple_of(i * 16, 16), 16)
+        values = raw[rows, :].astype(F32)
+        center = jnp.mean(values, axis=-1, keepdims=True)
+        spread = jnp.mean((values - center) * (values - center), axis=-1, keepdims=True)
+        T[own, rows, :] = (
+            (values - center) * lax.rsqrt(spread + 1e-06) * gain[...] + bias[...]
+        ).astype(BF)
+
     pl.semaphore_wait(barrier, len(peers))
 
     sent = []
@@ -82,10 +99,31 @@
         sent.append(copy)
         return copy
 
+    def part(seg, yy):
+        return pl.ds(pl.multiple_of(seg + yy * GROWS, GROWS), GROWS)
+
     wo_cross = send(
-        wo_hbm.at[my_rows], WO.at[pl.ds(own_seg + y * GROWS, GROWS)],
-        wos.at[0], wor.at[0], cross,
+        wo_hbm.at[part(0, y)], WO.at[part(own_seg, y)], wos.at[0], wor.at[0], cross
     )
+
+    def quarter(h, q):
+        return pl.ds(h * HALF + q * QUART, QUART)
+
+    zcopy, xcopy = {}, {}
+
+    def zsend(step, h, q, s):
+        ref = T.at[s, quarter(h, q)]
+        zcopy[step, h, q] = send(ref, ref, zs.at[step, h, q], zr.at[step, h, q], zdev[h])
+
+    def xsend(step, h, q, s):
+        ref = T.at[s, quarter(h, q)]
+        xcopy[step, h] = send(ref, ref, xs.at[step, h], xr.at[step, h], x2)
+
+    sign = (1, -1)
+    for q in range(2):
+        for h in range(2):
+            zsend(0, h, q, own)
+
     wq_mate = [
         send(wq_hbm.at[j], WQ.at[c * 3 + j], wqs.at[j], wqr.at[j], mate) for j in range(3)
     ]
@@ -95,40 +133,6 @@
         rows = pl.ds(pl.multiple_of(lax.rem(y + k + 1, NY) * GROWS, GROWS), GROWS)
         g_rs.append(send(g_hbm.at[rows], GR.at[k], gs.at[k], gr.at[k], ydev[k]))
 
-    def slot(col, zz):
-        return col * NZ + lax.rem(zz + 2 * NZ, NZ)
-
-    def quarter(h, q):
-        return pl.ds(h * HALF + q * QUART, QUART)
-
-    zcopy, xcopy = {}, {}
-
-    def zsend(step, h, q, s):
-        ref = T.at[s, quarter(h, q)]
-        zcopy[step, h, q] = send(ref, ref, zs.at[h, step, q], zr.at[h, step, q], zdev[h])
-
-    def xsend(step, h, q, s):
-        ref = T.at[s, quarter(h, q)]
-        xcopy[step, h, q] = send(ref, ref, xs.at[step, h, q], xr.at[step, h, q], x2)
-
-    sign = (1, -1)
-    own = slot(xh, z)
-
-    load_raw.wait()
-    for q in range(2):
-        for h in range(2):
-            @pl.loop(0, QUART // 16)
-            def _(i, h=h, q=q):
-                rows = pl.ds(pl.multiple_of(h * HALF + q * QUART + i * 16, 16), 16)
-                values = raw[rows, :].astype(F32)
-                center = jnp.mean(values, axis=-1, keepdims=True)
-                spread = jnp.mean((values - center) * (values - center), axis=-1, keepdims=True)
-                T[own, rows, :] = (
-                    (values - center) * lax.rsqrt(spread + 1e-06) * gain[...] + bias[...]
-                ).astype(BF)
-            zsend(0, h, q, own)
-            xsend(0, h, q, own)
-
     def project(s, base, count):
         @pl.loop(0, count)
         def _(j):
@@ -148,6 +152,11 @@
         zz = lax.rem(z + k, NZ)
         ccopy[k] = send(CTX.at[slot(1 - xh, z + k)], CTXR.at[zz], cs.at[k], cr.at[k], x2)
 
+    def by_rows(count, fn):
+        @pl.loop(0, count // 16)
+        def _(i):
+            fn(pl.ds(pl.multiple_of(i * 16, 16), 16))
+
     for copy in load_wq:
         copy.wait()
     project(own, c * 3, 3)
@@ -158,53 +167,42 @@
         copy.wait_recv()
     project(own, (1 - c) * 3, 3)
     attention(own)
+
+    wo_cross.wait_recv()
+    for h in range(2):
+        xsend(0, h, 1, own)
+    rows = WO.at[part(far_seg, y)]
+    wo_y = [send(rows, rows, wos.at[2 + k], wor.at[2 + k], ydev[k]) for k in range(3)]
+    wo_fwd = [send(rows, rows, wos.at[5], wor.at[5], mate)]
+
     for h in range(2):
         zcopy[0, h, 1].wait_recv()
         zsend(1, h, 1, slot(xh, z - sign[h]))
-
-    wo_cross.wait_recv()
-    far_rows = WO.at[pl.ds(far_seg + y * GROWS, GROWS)]
-    wo_y = [send(far_rows, far_rows, wos.at[2 + k], wor.at[2 + k], ydev[k]) for k in range(3)]
-    wo_fwd = [send(far_rows, far_rows, wos.at[5], wor.at[5], mate)]
-
-    for q in range(2):
-        for h in range(2):
-            zcopy[1, h, q].wait_recv()
-            zsend(2, h, q, slot(xh, z + 2))
-            xsend(1, h, q, slot(xh, z + 2))
-    for q in range(2):
-        for h in range(2):
-            xcopy[0, h, q].wait_recv()
-            zsend(3, h, q, slot(1 - xh, z))
-
-    @pl.loop(0, 2)
-    def _(i):
-        s = jnp.where(i == 0, slot(1 - xh, z), slot(xh, z + 2))
-        project(s, 0, 6)
-        attention(s)
-    ctx_send(0)
-
+    for h in range(2):
+        zcopy[1, h, 0].wait_recv()
+        zsend(2, h, 0, slot(xh, z + 2))
+        xsend(1, h, 0, slot(xh, z + 2))
+    for h in range(2):
+        xsend(2, h, 0, slot(xh, z - sign[h]))
+    for h in range(2):
+        zcopy[1, h, 1].wait_recv()
+        xcopy[0, h].wait_recv()
+        zsend(3, h, 1, slot(1 - xh, z))
+        zsend(2, h, 1, slot(xh, z + 2))
+    project(slot(xh, z + 2), 0, 6)
+    attention(slot(xh, z + 2))
+
+    for h in range(2):
+        zcopy[3, h, 1].wait_recv()
+        zsend(4, h, 1, slot(1 - xh, z - sign[h]))
+    for h in range(2):
+        xcopy[1, h].wait_recv()
+        zsend(3, h, 0, slot(1 - xh, z + 2))
     for q in range(2):
         for h in range(2):
             zcopy[2, h, q].wait_recv()
-    for h in range(2):
-        xcopy[1, h, 0].wait_recv()
-        zsend(4, h, 0, slot(1 - xh, z + 2))
-
-    @pl.loop(0, 2)
-    def _(i):
-        s = slot(xh, z + 1 + 2 * i)
-        project(s, 0, 6)
-        attention(s)
-
-    for h in range(2):
-        xcopy[1, h, 1].wait_recv()
-        zsend(4, h, 1, slot(1 - xh, z + 2))
-
-    def by_rows(count, fn):
-        @pl.loop(0, count // 16)
-        def _(i):
-            fn(pl.ds(pl.multiple_of(i * 16, 16), 16))
+    project(slot(xh, z + 1), 0, 6)
+    attention(slot(xh, z + 1))
 
     load_g.wait()
     for copy in g_rs:
@@ -218,14 +216,19 @@
     by_rows(GROWS, sum4)
     g_x = send(GX, GXR, gs.at[3], gr.at[3], xlo)
 
-    for k in range(3):
-        wo_y[k].wait_recv()
-        rows = WO.at[pl.ds(far_seg + lax.rem(y + NY - k - 1, NY) * GROWS, GROWS)]
-        wo_fwd.append(send(rows, rows, wos.at[6 + k], wor.at[6 + k], mate))
-
+    for h in range(2):
+        zcopy[4, h, 1].wait_recv()
+        zsend(5, h, 1, slot(1 - xh, z + 2))
     project(slot(1 - xh, z + 2), 0, 6)
     attention(slot(1 - xh, z + 2))
     ctx_send(2)
+
+    for k in range(3):
+        wo_y[k].wait_recv()
+        rows = WO.at[part(far_seg, lax.rem(y + NY - k - 1, NY))]
+        wo_fwd.append(send(rows, rows, wos.at[6 + k], wor.at[6 + k], mate))
+    project(slot(xh, z + 3), 0, 6)
+    attention(slot(xh, z + 3))
 
     load_wo.wait()
     wo_mate.wait_recv()
@@ -245,16 +248,6 @@
                 + jnp.dot(CTXR[zz], WO[far, cols], preferred_element_type=F32)
             ).astype(BF)
 
-    ccopy[0].wait_recv()
-    out_project(0)
-
-    g_x.wait_recv()
-
-    def sum2(rows):
-        GT[rows, :] = (GX[rows, :].astype(F32) + GXR[rows, :].astype(F32)).astype(BF)
-    by_rows(GROWS, sum2)
-    g_ag = [send(GT, GA.at[k], gs.at[4 + k], gr.at[4 + k], ydev[k]) for k in range(3)]
-
     ccopy[2].wait_recv()
     out_project(2)
 
@@ -271,14 +264,24 @@
         rsend(0, q, z + 2, 0, 1)
         rsend(1, q, z + 2, 1, 0)
 
-    for q in range(2):
-        for h in range(2):
-            zcopy[3, h, q].wait_recv()
-            zcopy[4, h, q].wait_recv()
+    for h in range(2):
+        zcopy[3, h, 0].wait_recv()
+        zcopy[5, h, 1].wait_recv()
+        xcopy[2, h].wait_recv()
     for k in (1, 3):
         project(slot(1 - xh, z + k), 0, 6)
         attention(slot(1 - xh, z + k))
         ctx_send(k)
+    for h in range(2):
+        xsend(3, h, 0, own)
+
+    g_x.wait_recv()
+
+    def sum2(rows):
+        GT[rows, :] = (GX[rows, :].astype(F32) + GXR[rows, :].astype(F32)).astype(BF)
+    by_rows(GROWS, sum2)
+    g_ag = [send(GT, GA.at[k], gs.at[4 + k], gr.at[4 + k], ydev[k]) for k in range(3)]
+
     ccopy[1].wait_recv()
     out_project(1)
     for q in range(2):
@@ -302,19 +305,19 @@
                 ).astype(BF)
             rsend(2 + h, q, z - sign[h], h, 1 - h)
 
-    written = []
-    for k in range(4):
-        if k:
-            g_ag[k - 1].wait_recv()
-        if k >= 2:
-            written[k - 2].wait()
-
-        def widen(rows, k=k):
-            part = GT[rows, :] if k == 0 else GA[k - 1, rows, :]
-            GF[k % 2, rows, :] = part.astype(F32)
-        by_rows(GROWS, widen)
-        rows = pl.ds(pl.multiple_of(lax.rem(y + NY - k, NY) * GROWS, GROWS), GROWS)
-        written.append(local(GF.at[k % 2], gsum_hbm.at[rows], outs.at[k]))
+    for h in range(2):
+        xcopy[3, h].wait_recv()
+    project(slot(1 - xh, z), 0, 6)
+    attention(slot(1 - xh, z))
+    ctx_send(0)
+    ccopy[0].wait_recv()
+    out_project(0)
+
+    written = [local(GT, gsum_hbm.at[my_rows], outs.at[0])]
+    for k in range(3):
+        g_ag[k].wait_recv()
+        rows = pl.ds(pl.multiple_of(lax.rem(y + NY - k - 1, NY) * GROWS, GROWS), GROWS)
+        written.append(local(GA.at[k], gsum_hbm.at[rows], outs.at[1 + k]))
 
     for q in range(2):
         for h in range(2):
@@ -333,10 +336,43 @@
             written.append(
                 local(OM.at[quarter(h, q)], mixed_hbm.at[quarter(h, q)], outs.at[4 + h * 2 + q])
             )
-    for copy in written[2:]:
+    for copy in written:
         copy.wait()
     for copy in sent:
         copy.wait_send()
+
+
+NG = 8
+NM = 2
+
+
+def finish(mixed_in, grad_in, mixed_out, grad_out, held, narrow, wide, isem, osem):
+    def chunk(n, i, total):
+        return pl.ds(i * (total // n), total // n)
+
+    def copy(src, dst, sem):
+        made = pltpu.make_async_copy(src, dst, sem)
+        made.start()
+        return made
+
+    grads = [chunk(NG, i, WIDTH) for i in range(NG)]
+    rows = [chunk(NM, i, SEQ) for i in range(NM)]
+    came = [copy(grad_in.at[r], narrow.at[r], isem.at[i]) for i, r in enumerate(grads)]
+    came += [copy(mixed_in.at[r], held.at[r], isem.at[NG + i]) for i, r in enumerate(rows)]
+    left = []
+    for i, r in enumerate(grads):
+        came[i].wait()
+
+        @pl.loop(0, WIDTH // NG // 16)
+        def _(j, i=i):
+            at = pl.ds(pl.multiple_of(i * (WIDTH // NG) + j * 16, 16), 16)
+            wide[at, :] = narrow[at, :].astype(F32)
+        left.append(copy(wide.at[r], grad_out.at[r], osem.at[i]))
+    for i, r in enumerate(rows):
+        came[NG + i].wait()
+        left.append(copy(held.at[r], mixed_out.at[r], osem.at[NG + i]))
+    for made in left:
+        made.wait()
 
 
 def body(tokens, ln_gain, ln_bias, w_qkv, w_out, grad_partial):
@@ -347,7 +383,7 @@
         kernel,
         out_shape=(
             jax.ShapeDtypeStruct((SEQ, D), BF),
-            jax.ShapeDtypeStruct((WIDTH, D), F32),
+            jax.ShapeDtypeStruct((WIDTH, D), BF),
         ),
         in_specs=[any_spec, vmem, vmem, any_spec, any_spec, any_spec],
         out_specs=(any_spec, any_spec),
@@ -367,10 +403,9 @@
             pltpu.VMEM((GROWS, D), BF),
             pltpu.VMEM((GROWS, D), BF),
             pltpu.VMEM((3, GROWS, D), BF),
-            pltpu.VMEM((2, GROWS, D), F32),
             pltpu.VMEM((SEQ, D), BF),
-            dma((2, 5, 2)), dma((2, 5, 2)),
-            dma((2, 2, 2)), dma((2, 2, 2)),
+            dma((6, 2, 2)), dma((6, 2, 2)),
+            dma((4, 2)), dma((4, 2)),
             dma((4,)), dma((4,)),
             dma((6, 2)), dma((6, 2)),
             dma((3,)), dma((3,)),
@@ -385,6 +420,21 @@
         tokens[0], ln_gain[None], ln_bias[None],
         jnp.transpose(w_qkv, (1, 0, 2)), w_out, grad_partial[0],
     )
+    mixed, grad_sum = pl.pallas_call(
+        finish,
+        out_shape=(
+            jax.ShapeDtypeStruct((SEQ, D), BF),
+            jax.ShapeDtypeStruct((WIDTH, D), F32),
+        ),
+        in_specs=[any_spec, any_spec],
+        out_specs=(any_spec, any_spec),
+        scratch_shapes=[
+            pltpu.VMEM((SEQ, D), BF),
+            pltpu.VMEM((WIDTH, D), BF),
+            pltpu.VMEM((WIDTH, D), F32),
+            dma((NG + NM,)), dma((NG + NM,)),
+        ],
+    )(mixed, grad_sum)
     return (mixed[None], grad_sum)
 
 

time: 160 us -> 140 us (0.88)
  Pallas kernels: 151 us -> 139 us
  local copies, waits for them, and re-layouts: 7.87 us -> 0 us
    pallas_call x1, Pallas kernels: 151 us -> 135 us  [body(): pl.pallas_call(kernel, out_shape=(jax.ShapeDtypeStruct((SEQ, D), BF), jax...]
    unnamed x2 -> x0, local copies, waits for them, and re-layouts: 7.87 us -> none
    pallas_call x0 -> x1, Pallas kernels: none -> 3.93 us  [body(): pl.pallas_call(finish, out_shape=(jax.ShapeDtypeStruct((SEQ, D), BF), jax...]
where the time goes in v2:
time: 140 us
  Pallas kernels  139 us (99%)
    pallas_call x1, Pallas kernels, body(): pl.pallas_call(kernel, out_shape=(jax.ShapeDtypeStruct((SEQ, D), BF), jax...  135 us
    pallas_call x1, Pallas kernels, body(): pl.pallas_call(finish, out_shape=(jax.ShapeDtypeStruct((SEQ, D), BF), jax...  3.93 us

profile of v2, /device:TPU:0, one launch (start us, length us, event | category | flops | bytes accessed | tf_op | source)
XLA Modules:
  0.0 139.8 jit_solution(8913961722543265578)
XLA Ops:
  0.6 135.2 %shard_map.77 = (bf16[128,5120]{1,0:T(8,128)(2,1)}, bf16[256,5120]{1,0:T(8,128)(2,1)}) custom-call(bf16[128,5120]{1,0:T(8,128)(2,1)} %bitcast.8, f32[1,5120]{1,0:T(1,128)} %bitcast.9, f32[1,5120]{1,0:T(1,128)} %bitcast.10, bf16[3,5120,256]{2,1,0:T(8,128)(2,1)} %bitcast.6, bf16[256,5120]{1,0:T(8,128)(2,1)} %wo_hbm.1, bf16[256,5120]{1,0:T(8,128)(2,1)} %bitcast.7), custom_call_target="tpu_custom_call" | custom-call | tf_op jit(solution)/shard_map/pallas_call | solution.py:382
  135.9 3.9 %shard_map.78 = (bf16[128,5120]{1,0:T(8,128)(2,1)}, f32[256,5120]{1,0:T(8,128)}) custom-call(bf16[128,5120]{1,0:T(8,128)(2,1)} %get-tuple-element.6.mixed_in, bf16[256,5120]{1,0:T(8,128)(2,1)} %get-tuple-element.7.grad_in), custom_call_target="tpu_custom_call" | custom-call | tf_op jit(solution)/shard_map/pallas_call | solution.py:423

commit v3 on v2

--- a/solution.py
+++ b/solution.py
@@ -57,7 +57,13 @@
         copy.start()
         return copy
 
-    load_raw = local(tok_hbm, raw, loc.at[0])
+    def quarter(h, q):
+        return pl.ds(h * HALF + q * QUART, QUART)
+
+    load_raw = [
+        [local(tok_hbm.at[quarter(h, q)], raw.at[quarter(h, q)], loc.at[6 + 2 * q + h]) for h in range(2)]
+        for q in range(2)
+    ]
     load_wq = [local(wq_hbm.at[j], WQ.at[c * 3 + j], loc.at[1 + j]) for j in range(3)]
     own_seg = pl.multiple_of((xh * 2 + c) * WIDTH, WIDTH)
     far_seg = pl.multiple_of(((1 - xh) * 2 + c) * WIDTH, WIDTH)
@@ -74,18 +80,6 @@
         return col * NZ + lax.rem(zz + 2 * NZ, NZ)
 
     own = slot(xh, z)
-    load_raw.wait()
-
-    @pl.loop(0, SEQ // 16)
-    def _(i):
-        rows = pl.ds(pl.multiple_of(i * 16, 16), 16)
-        values = raw[rows, :].astype(F32)
-        center = jnp.mean(values, axis=-1, keepdims=True)
-        spread = jnp.mean((values - center) * (values - center), axis=-1, keepdims=True)
-        T[own, rows, :] = (
-            (values - center) * lax.rsqrt(spread + 1e-06) * gain[...] + bias[...]
-        ).astype(BF)
-
     pl.semaphore_wait(barrier, len(peers))
 
     sent = []
@@ -106,24 +100,6 @@
         wo_hbm.at[part(0, y)], WO.at[part(own_seg, y)], wos.at[0], wor.at[0], cross
     )
 
-    def quarter(h, q):
-        return pl.ds(h * HALF + q * QUART, QUART)
-
-    zcopy, xcopy = {}, {}
-
-    def zsend(step, h, q, s):
-        ref = T.at[s, quarter(h, q)]
-        zcopy[step, h, q] = send(ref, ref, zs.at[step, h, q], zr.at[step, h, q], zdev[h])
-
-    def xsend(step, h, q, s):
-        ref = T.at[s, quarter(h, q)]
-        xcopy[step, h] = send(ref, ref, xs.at[step, h], xr.at[step, h], x2)
-
-    sign = (1, -1)
-    for q in range(2):
-        for h in range(2):
-            zsend(0, h, q, own)
-
     wq_mate = [
         send(wq_hbm.at[j], WQ.at[c * 3 + j], wqs.at[j], wqr.at[j], mate) for j in range(3)
     ]
@@ -152,6 +128,32 @@
         zz = lax.rem(z + k, NZ)
         ccopy[k] = send(CTX.at[slot(1 - xh, z + k)], CTXR.at[zz], cs.at[k], cr.at[k], x2)
 
+    zcopy, xcopy = {}, {}
+
+    def zsend(step, h, q, s):
+        ref = T.at[s, quarter(h, q)]
+        zcopy[step, h, q] = send(ref, ref, zs.at[step, h, q], zr.at[step, h, q], zdev[h])
+
+    def xsend(step, h, q, s):
+        ref = T.at[s, quarter(h, q)]
+        xcopy[step, h] = send(ref, ref, xs.at[step, h], xr.at[step, h], x2)
+
+    sign = (1, -1)
+    for q in range(2):
+        for h in range(2):
+            load_raw[q][h].wait()
+
+            @pl.loop(0, QUART // 16)
+            def _(i, h=h, q=q):
+                rows = pl.ds(pl.multiple_of(h * HALF + q * QUART + i * 16, 16), 16)
+                values = raw[rows, :].astype(F32)
+                center = jnp.mean(values, axis=-1, keepdims=True)
+                spread = jnp.mean((values - center) * (values - center), axis=-1, keepdims=True)
+                T[own, rows, :] = (
+                    (values - center) * lax.rsqrt(spread + 1e-06) * gain[...] + bias[...]
+                ).astype(BF)
+            zsend(0, h, q, own)
+
     def by_rows(count, fn):
         @pl.loop(0, count // 16)
         def _(i):
@@ -183,8 +185,6 @@
         zsend(2, h, 0, slot(xh, z + 2))
         xsend(1, h, 0, slot(xh, z + 2))
     for h in range(2):
-        xsend(2, h, 0, slot(xh, z - sign[h]))
-    for h in range(2):
         zcopy[1, h, 1].wait_recv()
         xcopy[0, h].wait_recv()
         zsend(3, h, 1, slot(1 - xh, z))
@@ -192,18 +192,6 @@
     project(slot(xh, z + 2), 0, 6)
     attention(slot(xh, z + 2))
 
-    for h in range(2):
-        zcopy[3, h, 1].wait_recv()
-        zsend(4, h, 1, slot(1 - xh, z - sign[h]))
-    for h in range(2):
-        xcopy[1, h].wait_recv()
-        zsend(3, h, 0, slot(1 - xh, z + 2))
-    for q in range(2):
-        for h in range(2):
-            zcopy[2, h, q].wait_recv()
-    project(slot(xh, z + 1), 0, 6)
-    attention(slot(xh, z + 1))
-
     load_g.wait()
     for copy in g_rs:
         copy.wait_recv()
@@ -214,7 +202,26 @@
             + (GR[1, rows, :].astype(F32) + GR[2, rows, :].astype(F32))
         ).astype(BF)
     by_rows(GROWS, sum4)
-    g_x = send(GX, GXR, gs.at[3], gr.at[3], xlo)
+    g_half = [pl.ds(i * (GROWS // 2), GROWS // 2) for i in range(2)]
+
+    def g_swap(i):
+        return send(GX.at[g_half[i]], GXR.at[g_half[i]], gs.at[3 + i], gr.at[3 + i], xlo)
+
+    g_x = [g_swap(0)]
+    for h in range(2):
+        xsend(2, h, 0, slot(xh, z - sign[h]))
+
+    for h in range(2):
+        zcopy[3, h, 1].wait_recv()
+        zsend(4, h, 1, slot(1 - xh, z - sign[h]))
+    for h in range(2):
+        xcopy[1, h].wait_recv()
+        zsend(3, h, 0, slot(1 - xh, z + 2))
+    for q in range(2):
+        for h in range(2):
+            zcopy[2, h, q].wait_recv()
+    project(slot(xh, z + 1), 0, 6)
+    attention(slot(xh, z + 1))
 
     for h in range(2):
         zcopy[4, h, 1].wait_recv()
@@ -222,6 +229,7 @@
     project(slot(1 - xh, z + 2), 0, 6)
     attention(slot(1 - xh, z + 2))
     ctx_send(2)
+    g_x.append(g_swap(1))
 
     for k in range(3):
         wo_y[k].wait_recv()
@@ -275,12 +283,13 @@
     for h in range(2):
         xsend(3, h, 0, own)
 
-    g_x.wait_recv()
+    for copy in g_x:
+        copy.wait_recv()
 
     def sum2(rows):
         GT[rows, :] = (GX[rows, :].astype(F32) + GXR[rows, :].astype(F32)).astype(BF)
     by_rows(GROWS, sum2)
-    g_ag = [send(GT, GA.at[k], gs.at[4 + k], gr.at[4 + k], ydev[k]) for k in range(3)]
+    g_ag = [send(GT, GA.at[k], gs.at[5 + k], gr.at[5 + k], ydev[k]) for k in range(3)]
 
     ccopy[1].wait_recv()
     out_project(1)
@@ -312,6 +321,9 @@
     ctx_send(0)
     ccopy[0].wait_recv()
     out_project(0)
+
+    for copy in sent[:-9]:
+        copy.wait_send()
 
     written = [local(GT, gsum_hbm.at[my_rows], outs.at[0])]
     for k in range(3):
@@ -338,7 +350,7 @@
             )
     for copy in written:
         copy.wait()
-    for copy in sent:
+    for copy in sent[-9:]:
         copy.wait_send()
 
 
@@ -410,8 +422,8 @@
             dma((6, 2)), dma((6, 2)),
             dma((3,)), dma((3,)),
             dma((9,)), dma((9,)),
-            dma((7,)), dma((7,)),
-            dma((6,)), dma((8,)),
+            dma((8,)), dma((8,)),
+            dma((10,)), dma((8,)),
         ],
         compiler_params=pltpu.CompilerParams(
             collective_id=0, has_side_effects=True, vmem_limit_bytes=67043328

time: 140 us -> 133 us (0.950)
  Pallas kernels: 139 us -> 132 us
    pallas_call x1, Pallas kernels: 135 us -> 128 us  [body(): pl.pallas_call(kernel, out_shape=(jax.ShapeDtypeStruct((SEQ, D), BF), jax...]
where the time goes in v3:
time: 133 us; the launch traced here: 132 us
  Pallas kernels  132 us (99%)
    pallas_call x1, Pallas kernels, body(): pl.pallas_call(kernel, out_shape=(jax.ShapeDtypeStruct((SEQ, D), BF), jax...  128 us
    pallas_call x1, Pallas kernels, body(): pl.pallas_call(finish, out_shape=(jax.ShapeDtypeStruct((SEQ, D), BF), jax...  3.93 us

profile of v3, /device:TPU:0, one launch (start us, length us, event | category | flops | bytes accessed | tf_op | source)
XLA Modules:
  0.0 132.4 jit_solution(16889099557459112535)
XLA Ops:
  0.6 127.8 %shard_map.77 = (bf16[128,5120]{1,0:T(8,128)(2,1)}, bf16[256,5120]{1,0:T(8,128)(2,1)}) custom-call(bf16[128,5120]{1,0:T(8,128)(2,1)} %bitcast.8, f32[1,5120]{1,0:T(1,128)} %bitcast.9, f32[1,5120]{1,0:T(1,128)} %bitcast.10, bf16[3,5120,256]{2,1,0:T(8,128)(2,1)} %bitcast.6, bf16[256,5120]{1,0:T(8,128)(2,1)} %wo_hbm.1, bf16[256,5120]{1,0:T(8,128)(2,1)} %bitcast.7), custom_call_target="tpu_custom_call" | custom-call | tf_op jit(solution)/shard_map/pallas_call | solution.py:394
  128.4 3.9 %shard_map.78 = (bf16[128,5120]{1,0:T(8,128)(2,1)}, f32[256,5120]{1,0:T(8,128)}) custom-call(bf16[128,5120]{1,0:T(8,128)(2,1)} %get-tuple-element.6.mixed_in, bf16[256,5120]{1,0:T(8,128)(2,1)} %get-tuple-element.7.grad_in), custom_call_target="tpu_custom_call" | custom-call | tf_op jit(solution)/shard_map/pallas_call | solution.py:435

commit v4 on v3

--- a/solution.py
+++ b/solution.py
@@ -31,11 +31,11 @@
 
 def kernel(
     tok_hbm, gain, bias, wq_hbm, wo_hbm, g_hbm,
-    mixed_hbm, gsum_hbm,
+    OM, gsum,
     raw, T, WQ, WO, QKV, CTX, CTXR, PS, RB,
-    GO, GR, GX, GXR, GT, GA, OM,
+    GO, GR, GX, GXR, GT, GA,
     zs, zr, xs, xr, cs, cr, rss, rsr,
-    wqs, wqr, wos, wor, gs, gr, loc, outs,
+    wqs, wqr, wos, wor, gs, gr, loc,
 ):
     dp = lax.axis_index("dp")
     mp = lax.axis_index("mp")
@@ -51,6 +51,11 @@
     cross = dev(y, 1 - xl, 1 - xh, z, c)
     xlo = dev(y, 1 - xl, xh, z, c)
     ydev = [dev(y + k, xl, xh, z, c) for k in (1, 2, 3 - NY)]
+
+    barrier = pltpu.get_barrier_semaphore()
+    peers = [*zdev, x2, mate, cross, xlo, *ydev]
+    for peer in peers:
+        pl.semaphore_signal(barrier, inc=1, device_id=peer, device_id_type=MESH)
 
     def local(src, dst, sem):
         copy = pltpu.make_async_copy(src, dst, sem)
@@ -71,15 +76,25 @@
     my_rows = pl.ds(pl.multiple_of(y * GROWS, GROWS), GROWS)
     load_g = local(g_hbm.at[my_rows], GO, loc.at[5])
 
-    barrier = pltpu.get_barrier_semaphore()
-    peers = [*zdev, x2, mate, cross, xlo, *ydev]
-    for peer in peers:
-        pl.semaphore_signal(barrier, inc=1, device_id=peer, device_id_type=MESH)
-
     def slot(col, zz):
         return col * NZ + lax.rem(zz + 2 * NZ, NZ)
 
     own = slot(xh, z)
+    def norm_rows(h, q):
+        load_raw[q][h].wait()
+
+        @pl.loop(0, QUART // 16)
+        def _(i):
+            rows = pl.ds(pl.multiple_of(h * HALF + q * QUART + i * 16, 16), 16)
+            values = raw[rows, :].astype(F32)
+            center = jnp.mean(values, axis=-1, keepdims=True)
+            spread = jnp.mean((values - center) * (values - center), axis=-1, keepdims=True)
+            T[own, rows, :] = (
+                (values - center) * lax.rsqrt(spread + 1e-06) * gain[...] + bias[...]
+            ).astype(BF)
+
+    for h in range(2):
+        norm_rows(h, 0)
     pl.semaphore_wait(barrier, len(peers))
 
     sent = []
@@ -100,6 +115,19 @@
         wo_hbm.at[part(0, y)], WO.at[part(own_seg, y)], wos.at[0], wor.at[0], cross
     )
 
+    zcopy, xcopy = {}, {}
+
+    def zsend(step, h, q, s):
+        ref = T.at[s, quarter(h, q)]
+        zcopy[step, h, q] = send(ref, ref, zs.at[step, h, q], zr.at[step, h, q], zdev[h])
+
+    def xsend(step, h, q, s):
+        ref = T.at[s, quarter(h, q)]
+        xcopy[step, h] = send(ref, ref, xs.at[step, h], xr.at[step, h], x2)
+
+    sign = (1, -1)
+    for h in range(2):
+        zsend(0, h, 0, own)
     wq_mate = [
         send(wq_hbm.at[j], WQ.at[c * 3 + j], wqs.at[j], wqr.at[j], mate) for j in range(3)
     ]
@@ -112,14 +140,28 @@
     def project(s, base, count):
         @pl.loop(0, count)
         def _(j):
-            QKV[base + j] = jnp.dot(T[s], WQ[base + j], preferred_element_type=F32).astype(BF)
-
-    def attention(s):
+            QKV[0, base + j] = jnp.dot(T[s], WQ[base + j], preferred_element_type=F32).astype(BF)
+
+    def project_pair(col, way):
+        up, down = slot(col, z + 1), slot(col, z + 3)
+        at_up, at_down = (1 - way) * HALF, way * HALF
+
+        @pl.loop(0, 6)
+        def _(j):
+            lhs = jnp.concatenate(
+                [T[up, at_up:at_up + HALF], T[down, at_down:at_down + HALF]], axis=0
+            )
+            both = jnp.dot(lhs, WQ[j], preferred_element_type=F32).astype(BF)
+            QKV[1, j, at_up:at_up + HALF] = both[:HALF]
+            QKV[2, j, at_down:at_down + HALF] = both[HALF:]
+
+    def attention(s, b=0):
         for cc in range(2):
             for h in range(2):
                 cols = slice(h * HEAD, (h + 1) * HEAD)
                 CTX[s, :, cc * WIDTH + h * HEAD:cc * WIDTH + (h + 1) * HEAD] = attend(
-                    QKV[cc * 3, :, cols], QKV[cc * 3 + 1, :, cols], QKV[cc * 3 + 2, :, cols]
+                    QKV[b, cc * 3, :, cols], QKV[b, cc * 3 + 1, :, cols],
+                    QKV[b, cc * 3 + 2, :, cols],
                 )
 
     ccopy = {}
@@ -127,32 +169,9 @@
     def ctx_send(k):
         zz = lax.rem(z + k, NZ)
         ccopy[k] = send(CTX.at[slot(1 - xh, z + k)], CTXR.at[zz], cs.at[k], cr.at[k], x2)
-
-    zcopy, xcopy = {}, {}
-
-    def zsend(step, h, q, s):
-        ref = T.at[s, quarter(h, q)]
-        zcopy[step, h, q] = send(ref, ref, zs.at[step, h, q], zr.at[step, h, q], zdev[h])
-
-    def xsend(step, h, q, s):
-        ref = T.at[s, quarter(h, q)]
-        xcopy[step, h] = send(ref, ref, xs.at[step, h], xr.at[step, h], x2)
-
-    sign = (1, -1)
-    for q in range(2):
-        for h in range(2):
-            load_raw[q][h].wait()
-
-            @pl.loop(0, QUART // 16)
-            def _(i, h=h, q=q):
-                rows = pl.ds(pl.multiple_of(h * HALF + q * QUART + i * 16, 16), 16)
-                values = raw[rows, :].astype(F32)
-                center = jnp.mean(values, axis=-1, keepdims=True)
-                spread = jnp.mean((values - center) * (values - center), axis=-1, keepdims=True)
-                T[own, rows, :] = (
-                    (values - center) * lax.rsqrt(spread + 1e-06) * gain[...] + bias[...]
-                ).astype(BF)
-            zsend(0, h, q, own)
+    for h in range(2):
+        norm_rows(h, 1)
+        zsend(0, h, 1, own)
 
     def by_rows(count, fn):
         @pl.loop(0, count // 16)
@@ -180,6 +199,7 @@
     for h in range(2):
         zcopy[0, h, 1].wait_recv()
         zsend(1, h, 1, slot(xh, z - sign[h]))
+    project_pair(xh, 0)
     for h in range(2):
         zcopy[1, h, 0].wait_recv()
         zsend(2, h, 0, slot(xh, z + 2))
@@ -220,8 +240,9 @@
     for q in range(2):
         for h in range(2):
             zcopy[2, h, q].wait_recv()
-    project(slot(xh, z + 1), 0, 6)
-    attention(slot(xh, z + 1))
+    project_pair(xh, 1)
+    attention(slot(xh, z + 1), 1)
+    attention(slot(xh, z + 3), 2)
 
     for h in range(2):
         zcopy[4, h, 1].wait_recv()
@@ -235,29 +256,43 @@
         wo_y[k].wait_recv()
         rows = WO.at[part(far_seg, lax.rem(y + NY - k - 1, NY))]
         wo_fwd.append(send(rows, rows, wos.at[6 + k], wor.at[6 + k], mate))
-    project(slot(xh, z + 3), 0, 6)
-    attention(slot(xh, z + 3))
+    for h in range(2):
+        xcopy[2, h].wait_recv()
+    project_pair(1 - xh, 0)
 
     load_wo.wait()
     wo_mate.wait_recv()
     for copy in wo_fwd:
         copy.wait_recv()
 
-    def out_project(k):
-        zz = lax.rem(z + k, NZ)
-        near = pl.ds(pl.multiple_of(xh * 2 * WIDTH, WIDTH), 2 * WIDTH)
-        far = pl.ds(pl.multiple_of((1 - xh) * 2 * WIDTH, WIDTH), 2 * WIDTH)
-
+    def out_tiles(fn):
         @pl.loop(0, D // 512)
         def _(j):
-            cols = pl.ds(pl.multiple_of(j * 512, 512), 512)
-            PS[zz, :, cols] = (
-                jnp.dot(CTX[slot(xh, zz)], WO[near, cols], preferred_element_type=F32)
-                + jnp.dot(CTXR[zz], WO[far, cols], preferred_element_type=F32)
+            fn(pl.ds(pl.multiple_of(j * 512, 512), 512))
+
+    near = pl.ds(pl.multiple_of(xh * 2 * WIDTH, WIDTH), 2 * WIDTH)
+    far = pl.ds(pl.multiple_of((1 - xh) * 2 * WIDTH, WIDTH), 2 * WIDTH)
+
+    def out_rows(pieces):
+        def joined(ref_at):
+            parts = [ref_at(k, start, count) for k, start, count in pieces]
+            return parts[0] if len(parts) == 1 else jnp.concatenate(parts, axis=0)
+
+        def tile(cols):
+            mine = joined(lambda k, start, count: CTX[slot(xh, z + k), start:start + count])
+            theirs = joined(lambda k, start, count: CTXR[lax.rem(z + k, NZ), start:start + count])
+            made = (
+                jnp.dot(mine, WO[near, cols], preferred_element_type=F32)
+                + jnp.dot(theirs, WO[far, cols], preferred_element_type=F32)
             ).astype(BF)
+            at = 0
+            for k, start, count in pieces:
+                PS[lax.rem(z + k, NZ), start:start + count, cols] = made[at:at + count]
+                at += count
+        out_tiles(tile)
 
     ccopy[2].wait_recv()
-    out_project(2)
+    out_rows([(2, 0, SEQ)])
 
     rcopy = {}
 
@@ -275,10 +310,9 @@
     for h in range(2):
         zcopy[3, h, 0].wait_recv()
         zcopy[5, h, 1].wait_recv()
-        xcopy[2, h].wait_recv()
+    project_pair(1 - xh, 1)
     for k in (1, 3):
-        project(slot(1 - xh, z + k), 0, 6)
-        attention(slot(1 - xh, z + k))
+        attention(slot(1 - xh, z + k), (k + 1) // 2)
         ctx_send(k)
     for h in range(2):
         xsend(3, h, 0, own)
@@ -292,13 +326,12 @@
     g_ag = [send(GT, GA.at[k], gs.at[5 + k], gr.at[5 + k], ydev[k]) for k in range(3)]
 
     ccopy[1].wait_recv()
-    out_project(1)
+    ccopy[3].wait_recv()
+    out_rows([(1, 0, HALF), (3, HALF, HALF)])
     for q in range(2):
         rsend(4, q, z + 1, 0, 0)
-    ccopy[3].wait_recv()
-    out_project(3)
-    for q in range(2):
         rsend(5, q, z - 1, 1, 1)
+    out_rows([(1, HALF, HALF), (3, 0, HALF)])
 
     for q in range(2):
         for h in range(2):
@@ -320,16 +353,20 @@
     attention(slot(1 - xh, z))
     ctx_send(0)
     ccopy[0].wait_recv()
-    out_project(0)
+    out_rows([(0, 0, SEQ)])
 
     for copy in sent[:-9]:
         copy.wait_send()
 
-    written = [local(GT, gsum_hbm.at[my_rows], outs.at[0])]
-    for k in range(3):
-        g_ag[k].wait_recv()
-        rows = pl.ds(pl.multiple_of(lax.rem(y + NY - k - 1, NY) * GROWS, GROWS), GROWS)
-        written.append(local(GA.at[k], gsum_hbm.at[rows], outs.at[1 + k]))
+    for k in range(4):
+        if k:
+            g_ag[k - 1].wait_recv()
+        base = lax.rem(y + NY - k, NY) * GROWS
+
+        def place(rows, k=k, base=base):
+            part = GT[rows, :] if k == 0 else GA[k - 1, rows, :]
+            gsum[pl.ds(pl.multiple_of(base + rows.start, 16), 16), :] = part.astype(F32)
+        by_rows(GROWS, place)
 
     for q in range(2):
         for h in range(2):
@@ -345,46 +382,19 @@
                     RB[2 + h, part, :].astype(F32) + RB[4 + h, part, :].astype(F32)
                 )
                 OM[rows, :] = (raw[rows, :].astype(F32) + proj).astype(BF)
-            written.append(
-                local(OM.at[quarter(h, q)], mixed_hbm.at[quarter(h, q)], outs.at[4 + h * 2 + q])
-            )
-    for copy in written:
-        copy.wait()
     for copy in sent[-9:]:
         copy.wait_send()
 
 
-NG = 8
-NM = 2
-
-
-def finish(mixed_in, grad_in, mixed_out, grad_out, held, narrow, wide, isem, osem):
-    def chunk(n, i, total):
-        return pl.ds(i * (total // n), total // n)
-
-    def copy(src, dst, sem):
-        made = pltpu.make_async_copy(src, dst, sem)
-        made.start()
-        return made
-
-    grads = [chunk(NG, i, WIDTH) for i in range(NG)]
-    rows = [chunk(NM, i, SEQ) for i in range(NM)]
-    came = [copy(grad_in.at[r], narrow.at[r], isem.at[i]) for i, r in enumerate(grads)]
-    came += [copy(mixed_in.at[r], held.at[r], isem.at[NG + i]) for i, r in enumerate(rows)]
-    left = []
-    for i, r in enumerate(grads):
-        came[i].wait()
-
-        @pl.loop(0, WIDTH // NG // 16)
-        def _(j, i=i):
-            at = pl.ds(pl.multiple_of(i * (WIDTH // NG) + j * 16, 16), 16)
-            wide[at, :] = narrow[at, :].astype(F32)
-        left.append(copy(wide.at[r], grad_out.at[r], osem.at[i]))
-    for i, r in enumerate(rows):
-        came[NG + i].wait()
-        left.append(copy(held.at[r], mixed_out.at[r], osem.at[NG + i]))
-    for made in left:
-        made.wait()
+def finish(mixed_in, grad_in, mixed_out, grad_out, sem):
+    made = [pltpu.make_async_copy(mixed_in, mixed_out, sem.at[4])]
+    for i in range(4):
+        rows = pl.ds(i * GROWS, GROWS)
+        made.append(pltpu.make_async_copy(grad_in.at[rows], grad_out.at[rows], sem.at[i]))
+    for copy in made:
+        copy.start()
+    for copy in made:
+        copy.wait()
 
 
 def body(tokens, ln_gain, ln_bias, w_qkv, w_out, grad_partial):
@@ -393,18 +403,15 @@
     vmem = pl.BlockSpec(memory_space=pltpu.VMEM)
     mixed, grad_sum = pl.pallas_call(
         kernel,
-        out_shape=(
-            jax.ShapeDtypeStruct((SEQ, D), BF),
-            jax.ShapeDtypeStruct((WIDTH, D), BF),
-        ),
+        out_shape=(pltpu.VMEM((SEQ, D), BF), pltpu.VMEM((WIDTH, D), F32)),
         in_specs=[any_spec, vmem, vmem, any_spec, any_spec, any_spec],
-        out_specs=(any_spec, any_spec),
+        out_specs=(vmem, vmem),
         scratch_shapes=[
             pltpu.VMEM((SEQ, D), BF),
             pltpu.VMEM((2 * NZ, SEQ, D), BF),
             pltpu.VMEM((6, D, WIDTH), BF),
             pltpu.VMEM((4 * WIDTH, D), BF),
-            pltpu.VMEM((6, SEQ, WIDTH), BF),
+            pltpu.VMEM((3, 6, SEQ, WIDTH), BF),
             pltpu.VMEM((2 * NZ, SEQ, 2 * WIDTH), BF),
             pltpu.VMEM((NZ, SEQ, 2 * WIDTH), BF),
             pltpu.VMEM((NZ, SEQ, D), BF),
@@ -415,7 +422,6 @@
             pltpu.VMEM((GROWS, D), BF),
             pltpu.VMEM((GROWS, D), BF),
             pltpu.VMEM((3, GROWS, D), BF),
-            pltpu.VMEM((SEQ, D), BF),
             dma((6, 2, 2)), dma((6, 2, 2)),
             dma((4, 2)), dma((4, 2)),
             dma((4,)), dma((4,)),
@@ -423,29 +429,27 @@
             dma((3,)), dma((3,)),
             dma((9,)), dma((9,)),
             dma((8,)), dma((8,)),
-            dma((10,)), dma((8,)),
+            dma((10,)),
         ],
         compiler_params=pltpu.CompilerParams(
-            collective_id=0, has_side_effects=True, vmem_limit_bytes=67043328
+            collective_id=0, has_side_effects=True, vmem_limit_bytes=57671680
         ),
     )(
         tokens[0], ln_gain[None], ln_bias[None],
         jnp.transpose(w_qkv, (1, 0, 2)), w_out, grad_partial[0],
     )
+    mixed = pltpu.with_memory_space_constraint(mixed, pltpu.VMEM)
+    grad_sum = pltpu.with_memory_space_constraint(grad_sum, pltpu.VMEM)
     mixed, grad_sum = pl.pallas_call(
         finish,
         out_shape=(
             jax.ShapeDtypeStruct((SEQ, D), BF),
             jax.ShapeDtypeStruct((WIDTH, D), F32),
         ),
-        in_specs=[any_spec, any_spec],
+        in_specs=[vmem, vmem],
         out_specs=(any_spec, any_spec),
-        scratch_shapes=[
-            pltpu.VMEM((SEQ, D), BF),
-            pltpu.VMEM((WIDTH, D), BF),
-            pltpu.VMEM((WIDTH, D), F32),
-            dma((NG + NM,)), dma((NG + NM,)),
-        ],
+        scratch_shapes=[dma((5,))],
+        compiler_params=pltpu.CompilerParams(vmem_limit_bytes=1 << 20),
     )(mixed, grad_sum)
     return (mixed[None], grad_sum)
 

time: 133 us -> 131 us (0.985)
  Pallas kernels: 132 us -> 130 us
where the time goes in v4:
time: 131 us
  Pallas kernels  130 us (99%)
    pallas_call x1, Pallas kernels, body(): pl.pallas_call(kernel, out_shape=(pltpu.VMEM((SEQ, D), BF), pltpu.VMEM((W...  127 us
    pallas_call x1, Pallas kernels, body(): pl.pallas_call(finish, out_shape=(jax.ShapeDtypeStruct((SEQ, D), BF), jax...  2.83 us

profile of v4, /device:TPU:0, one launch (start us, length us, event | category | flops | bytes accessed | tf_op | source)
XLA Modules:
  0.0 130.8 jit_solution(9138950786652851035)
XLA Ops:
  0.6 127.3 %shard_map.77 = (bf16[128,5120]{1,0:T(8,128)(2,1)S(1)}, f32[256,5120]{1,0:T(8,128)S(1)}) custom-call(bf16[128,5120]{1,0:T(8,128)(2,1)} %bitcast.8, f32[1,5120]{1,0:T(1,128)} %bitcast.9, f32[1,5120]{1,0:T(1,128)} %bitcast.10, bf16[3,5120,256]{2,1,0:T(8,128)(2,1)} %bitcast.6, bf16[256,5120]{1,0:T(8,128)(2,1)} %wo_hbm.1, bf16[256,5120]{1,0:T(8,128)(2,1)} %bitcast.7), custom_call_target="tpu_custom_call" | custom-call | tf_op jit(solution)/shard_map/pallas_call | solution.py:404
  128.0 2.8 %shard_map.78 = (bf16[128,5120]{1,0:T(8,128)(2,1)}, f32[256,5120]{1,0:T(8,128)}) custom-call(bf16[128,5120]{1,0:T(8,128)(2,1)S(1)} %get-tuple-element.6.mixed_in, f32[256,5120]{1,0:T(8,128)S(1)} %get-tuple-element.7.grad_in), custom_call_target="tpu_custom_call" | custom-call | tf_op jit(solution)/shard_map/pallas_call | solution.py:443

commit v5 on v4

--- a/solution.py
+++ b/solution.py
@@ -19,14 +19,20 @@
 F32 = jnp.float32
 
 
-def attend(query, keys, values):
-    scores = lax.dot_general(
-        query, keys, (((1,), (1,)), ((), ())), preferred_element_type=F32
-    ) * HEAD ** (-0.5)
-    scaled = scores - jnp.max(scores, axis=-1, keepdims=True)
-    expsc = jnp.exp(scaled)
-    attn = (expsc / jnp.sum(expsc, axis=-1, keepdims=True)).astype(BF)
-    return jnp.dot(attn, values, preferred_element_type=F32).astype(BF)
+def attend(heads):
+    scores = [
+        lax.dot_general(query, keys, (((1,), (1,)), ((), ())), preferred_element_type=F32)
+        * HEAD ** (-0.5)
+        for query, keys, _ in heads
+    ]
+    tops = [jnp.max(part, axis=-1, keepdims=True) for part in scores]
+    expsc = [jnp.exp(part - top) for part, top in zip(scores, tops)]
+    sums = [jnp.sum(part, axis=-1, keepdims=True) for part in expsc]
+    attn = [(part / total).astype(BF) for part, total in zip(expsc, sums)]
+    return [
+        jnp.dot(part, values, preferred_element_type=F32).astype(BF)
+        for part, (_, _, values) in zip(attn, heads)
+    ]
 
 
 def kernel(
@@ -155,20 +161,34 @@
             QKV[1, j, at_up:at_up + HALF] = both[:HALF]
             QKV[2, j, at_down:at_down + HALF] = both[HALF:]
 
-    def attention(s, b=0):
-        for cc in range(2):
-            for h in range(2):
-                cols = slice(h * HEAD, (h + 1) * HEAD)
-                CTX[s, :, cc * WIDTH + h * HEAD:cc * WIDTH + (h + 1) * HEAD] = attend(
-                    QKV[b, cc * 3, :, cols], QKV[b, cc * 3 + 1, :, cols],
-                    QKV[b, cc * 3 + 2, :, cols],
-                )
+    def attention(*units):
+        heads, places = [], []
+        for s, b, start, count in units:
+            rows = slice(start, start + count)
+            for cc in range(2):
+                for h in range(2):
+                    cols = slice(h * HEAD, (h + 1) * HEAD)
+                    heads.append((
+                        QKV[b, cc * 3, rows, cols], QKV[b, cc * 3 + 1, :, cols],
+                        QKV[b, cc * 3 + 2, :, cols],
+                    ))
+                    at = cc * WIDTH + h * HEAD
+                    places.append((s, rows, slice(at, at + HEAD)))
+        for place, made in zip(places, attend(heads)):
+            CTX[place] = made
+
+    def attend_all(s, b=0):
+        attention((s, b, 0, SEQ))
 
     ccopy = {}
 
-    def ctx_send(k):
-        zz = lax.rem(z + k, NZ)
-        ccopy[k] = send(CTX.at[slot(1 - xh, z + k)], CTXR.at[zz], cs.at[k], cr.at[k], x2)
+    def ctx_send(k, start=0, count=SEQ):
+        rows = pl.ds(start, count)
+        sems = (cs.at[k, start // HALF], cr.at[k, start // HALF])
+        ccopy[k, start] = send(
+            CTX.at[slot(1 - xh, z + k), rows], CTXR.at[lax.rem(z + k, NZ), rows], *sems, x2
+        )
+
     for h in range(2):
         norm_rows(h, 1)
         zsend(0, h, 1, own)
@@ -187,7 +207,7 @@
     for copy in wq_mate:
         copy.wait_recv()
     project(own, (1 - c) * 3, 3)
-    attention(own)
+    attend_all(own)
 
     wo_cross.wait_recv()
     for h in range(2):
@@ -210,7 +230,7 @@
         zsend(3, h, 1, slot(1 - xh, z))
         zsend(2, h, 1, slot(xh, z + 2))
     project(slot(xh, z + 2), 0, 6)
-    attention(slot(xh, z + 2))
+    attend_all(slot(xh, z + 2))
 
     load_g.wait()
     for copy in g_rs:
@@ -222,14 +242,14 @@
             + (GR[1, rows, :].astype(F32) + GR[2, rows, :].astype(F32))
         ).astype(BF)
     by_rows(GROWS, sum4)
-    g_half = [pl.ds(i * (GROWS // 2), GROWS // 2) for i in range(2)]
+    g_half = [pl.ds(0, 16), pl.ds(16, GROWS - 16)]
 
     def g_swap(i):
         return send(GX.at[g_half[i]], GXR.at[g_half[i]], gs.at[3 + i], gr.at[3 + i], xlo)
 
+    for h in range(2):
+        xsend(2, h, 0, slot(xh, z - sign[h]))
     g_x = [g_swap(0)]
-    for h in range(2):
-        xsend(2, h, 0, slot(xh, z - sign[h]))
 
     for h in range(2):
         zcopy[3, h, 1].wait_recv()
@@ -241,14 +261,14 @@
         for h in range(2):
             zcopy[2, h, q].wait_recv()
     project_pair(xh, 1)
-    attention(slot(xh, z + 1), 1)
-    attention(slot(xh, z + 3), 2)
+    attend_all(slot(xh, z + 1), 1)
+    attend_all(slot(xh, z + 3), 2)
 
     for h in range(2):
         zcopy[4, h, 1].wait_recv()
         zsend(5, h, 1, slot(1 - xh, z + 2))
     project(slot(1 - xh, z + 2), 0, 6)
-    attention(slot(1 - xh, z + 2))
+    attend_all(slot(1 - xh, z + 2))
     ctx_send(2)
     g_x.append(g_swap(1))
 
@@ -291,7 +311,7 @@
                 at += count
         out_tiles(tile)
 
-    ccopy[2].wait_recv()
+    ccopy[2, 0].wait_recv()
     out_rows([(2, 0, SEQ)])
 
     rcopy = {}
@@ -311,9 +331,11 @@
         zcopy[3, h, 0].wait_recv()
         zcopy[5, h, 1].wait_recv()
     project_pair(1 - xh, 1)
-    for k in (1, 3):
-        attention(slot(1 - xh, z + k), (k + 1) // 2)
-        ctx_send(k)
+    for turn in range(2):
+        halves = ((1, turn * HALF), (3, (1 - turn) * HALF))
+        attention(*[(slot(1 - xh, z + k), (k + 1) // 2, start, HALF) for k, start in halves])
+        for k, start in halves:
+            ctx_send(k, start, HALF)
     for h in range(2):
         xsend(3, h, 0, own)
 
@@ -325,12 +347,14 @@
     by_rows(GROWS, sum2)
     g_ag = [send(GT, GA.at[k], gs.at[5 + k], gr.at[5 + k], ydev[k]) for k in range(3)]
 
-    ccopy[1].wait_recv()
-    ccopy[3].wait_recv()
+    ccopy[1, 0].wait_recv()
+    ccopy[3, HALF].wait_recv()
     out_rows([(1, 0, HALF), (3, HALF, HALF)])
     for q in range(2):
         rsend(4, q, z + 1, 0, 0)
         rsend(5, q, z - 1, 1, 1)
+    ccopy[1, HALF].wait_recv()
+    ccopy[3, 0].wait_recv()
     out_rows([(1, HALF, HALF), (3, 0, HALF)])
 
     for q in range(2):
@@ -350,9 +374,9 @@
     for h in range(2):
         xcopy[3, h].wait_recv()
     project(slot(1 - xh, z), 0, 6)
-    attention(slot(1 - xh, z))
+    attend_all(slot(1 - xh, z))
     ctx_send(0)
-    ccopy[0].wait_recv()
+    ccopy[0, 0].wait_recv()
     out_rows([(0, 0, SEQ)])
 
     for copy in sent[:-9]:
@@ -424,7 +448,7 @@
             pltpu.VMEM((3, GROWS, D), BF),
             dma((6, 2, 2)), dma((6, 2, 2)),
             dma((4, 2)), dma((4, 2)),
-            dma((4,)), dma((4,)),
+            dma((4, 2)), dma((4, 2)),
             dma((6, 2)), dma((6, 2)),
             dma((3,)), dma((3,)),
             dma((9,)), dma((9,)),

time: 131 us -> 126 us (0.962)
  Pallas kernels: 130 us -> 125 us
    pallas_call x1, Pallas kernels: 127 us -> 122 us  [body(): pl.pallas_call(kernel, out_shape=(pltpu.VMEM((SEQ, D), BF), pltpu.VMEM((W...]
where the time goes in v5:
time: 126 us
  Pallas kernels  125 us (99%)
    pallas_call x1, Pallas kernels, body(): pl.pallas_call(kernel, out_shape=(pltpu.VMEM((SEQ, D), BF), pltpu.VMEM((W...  122 us
    pallas_call x1, Pallas kernels, body(): pl.pallas_call(finish, out_shape=(jax.ShapeDtypeStruct((SEQ, D), BF), jax...  2.83 us

profile of v5, /device:TPU:0, one launch (start us, length us, event | category | flops | bytes accessed | tf_op | source)
XLA Modules:
  0.0 125.9 jit_solution(17290774657790400555)
XLA Ops:
  0.6 122.5 %shard_map.77 = (bf16[128,5120]{1,0:T(8,128)(2,1)S(1)}, f32[256,5120]{1,0:T(8,128)S(1)}) custom-call(bf16[128,5120]{1,0:T(8,128)(2,1)} %bitcast.8, f32[1,5120]{1,0:T(1,128)} %bitcast.9, f32[1,5120]{1,0:T(1,128)} %bitcast.10, bf16[3,5120,256]{2,1,0:T(8,128)(2,1)} %bitcast.6, bf16[256,5120]{1,0:T(8,128)(2,1)} %wo_hbm.1, bf16[256,5120]{1,0:T(8,128)(2,1)} %bitcast.7), custom_call_target="tpu_custom_call" | custom-call | tf_op jit(solution)/shard_map/pallas_call | solution.py:428
  123.1 2.8 %shard_map.78 = (bf16[128,5120]{1,0:T(8,128)(2,1)}, f32[256,5120]{1,0:T(8,128)}) custom-call(bf16[128,5120]{1,0:T(8,128)(2,1)S(1)} %get-tuple-element.6.mixed_in, f32[256,5120]{1,0:T(8,128)S(1)} %get-tuple-element.7.grad_in), custom_call_target="tpu_custom_call" | custom-call | tf_op jit(solution)/shard_map/pallas_call | solution.py:467

commit v6 on v5

--- a/solution.py
+++ b/solution.py
@@ -242,14 +242,13 @@
             + (GR[1, rows, :].astype(F32) + GR[2, rows, :].astype(F32))
         ).astype(BF)
     by_rows(GROWS, sum4)
-    g_half = [pl.ds(0, 16), pl.ds(16, GROWS - 16)]
+    g_half = [pl.ds(0, 48), pl.ds(48, GROWS - 48)]
 
     def g_swap(i):
         return send(GX.at[g_half[i]], GXR.at[g_half[i]], gs.at[3 + i], gr.at[3 + i], xlo)
 
     for h in range(2):
         xsend(2, h, 0, slot(xh, z - sign[h]))
-    g_x = [g_swap(0)]
 
     for h in range(2):
         zcopy[3, h, 1].wait_recv()
@@ -270,7 +269,7 @@
     project(slot(1 - xh, z + 2), 0, 6)
     attend_all(slot(1 - xh, z + 2))
     ctx_send(2)
-    g_x.append(g_swap(1))
+    g_x = [g_swap(0)]
 
     for k in range(3):
         wo_y[k].wait_recv()
@@ -338,15 +337,24 @@
             ctx_send(k, start, HALF)
     for h in range(2):
         xsend(3, h, 0, own)
-
-    for copy in g_x:
-        copy.wait_recv()
-
-    def sum2(rows):
-        GT[rows, :] = (GX[rows, :].astype(F32) + GXR[rows, :].astype(F32)).astype(BF)
-    by_rows(GROWS, sum2)
-    g_ag = [send(GT, GA.at[k], gs.at[5 + k], gr.at[5 + k], ydev[k]) for k in range(3)]
-
+    g_x.append(g_swap(1))
+
+    g_ag = []
+
+    def g_share(i):
+        g_x[i].wait_recv()
+
+        @pl.loop(0, g_half[i].size // 16)
+        def _(j):
+            rows = pl.ds(pl.multiple_of(g_half[i].start + j * 16, 16), 16)
+            GT[rows, :] = (GX[rows, :].astype(F32) + GXR[rows, :].astype(F32)).astype(BF)
+        for k in range(3):
+            g_ag.append(send(
+                GT.at[g_half[i]], GA.at[k, g_half[i]],
+                gs.at[5 + 3 * i + k], gr.at[5 + 3 * i + k], ydev[k],
+            ))
+
+    g_share(0)
     ccopy[1, 0].wait_recv()
     ccopy[3, HALF].wait_recv()
     out_rows([(1, 0, HALF), (3, HALF, HALF)])
@@ -376,15 +384,17 @@
     project(slot(1 - xh, z), 0, 6)
     attend_all(slot(1 - xh, z))
     ctx_send(0)
+    g_share(1)
     ccopy[0, 0].wait_recv()
     out_rows([(0, 0, SEQ)])
 
-    for copy in sent[:-9]:
+    for copy in sent[:-12]:
         copy.wait_send()
 
     for k in range(4):
         if k:
             g_ag[k - 1].wait_recv()
+            g_ag[k + 2].wait_recv()
         base = lax.rem(y + NY - k, NY) * GROWS
 
         def place(rows, k=k, base=base):
@@ -406,7 +416,7 @@
                     RB[2 + h, part, :].astype(F32) + RB[4 + h, part, :].astype(F32)
                 )
                 OM[rows, :] = (raw[rows, :].astype(F32) + proj).astype(BF)
-    for copy in sent[-9:]:
+    for copy in sent[-12:]:
         copy.wait_send()
 
 
@@ -452,7 +462,7 @@
             dma((6, 2)), dma((6, 2)),
             dma((3,)), dma((3,)),
             dma((9,)), dma((9,)),
-            dma((8,)), dma((8,)),
+            dma((11,)), dma((11,)),
             dma((10,)),
         ],
         compiler_params=pltpu.CompilerParams(

time: 126 us -> 126 us (level)
  no operation moved by 1% of the time
where the time goes in v6:
time: 126 us
  Pallas kernels  125 us (99%)
    pallas_call x1, Pallas kernels, body(): pl.pallas_call(kernel, out_shape=(pltpu.VMEM((SEQ, D), BF), pltpu.VMEM((W...  123 us
    pallas_call x1, Pallas kernels, body(): pl.pallas_call(finish, out_shape=(jax.ShapeDtypeStruct((SEQ, D), BF), jax...  2.83 us

profile of v6, /device:TPU:0, one launch (start us, length us, event | category | flops | bytes accessed | tf_op | source)
XLA Modules:
  0.0 126.0 jit_solution(14788810926888661140)
XLA Ops:
  0.6 122.5 %shard_map.77 = (bf16[128,5120]{1,0:T(8,128)(2,1)S(1)}, f32[256,5120]{1,0:T(8,128)S(1)}) custom-call(bf16[128,5120]{1,0:T(8,128)(2,1)} %bitcast.8, f32[1,5120]{1,0:T(1,128)} %bitcast.9, f32[1,5120]{1,0:T(1,128)} %bitcast.10, bf16[3,5120,256]{2,1,0:T(8,128)(2,1)} %bitcast.6, bf16[256,5120]{1,0:T(8,128)(2,1)} %wo_hbm.1, bf16[256,5120]{1,0:T(8,128)(2,1)} %bitcast.7), custom_call_target="tpu_custom_call" | custom-call | tf_op jit(solution)/shard_map/pallas_call | solution.py:438
  123.2 2.8 %shard_map.78 = (bf16[128,5120]{1,0:T(8,128)(2,1)}, f32[256,5120]{1,0:T(8,128)}) custom-call(bf16[128,5120]{1,0:T(8,128)(2,1)S(1)} %get-tuple-element.6.mixed_in, f32[256,5120]{1,0:T(8,128)S(1)} %get-tuple-element.7.grad_in), custom_call_target="tpu_custom_call" | custom-call | tf_op jit(solution)/shard_map/pallas_call | solution.py:477
